TPU v7x, 128 devices: a whole 4x4x4 slice. The times are simulated.
128 devices in a mesh: rows: 8 (over z, y_hi), snaps: 16 (over x, y_lo, core).
Axes of the slice: x: 4, y: 4 (y_hi: 2, y_lo: 2; y = y_hi * 2 + y_lo), z: 4, core: 2. Of those that a mesh axis runs over, the one named last changes fastest.
Arguments:
- snapshots: float32 [16384, 4096], P('rows', 'snaps'), may hold values from -6 to 6
- weights: float32 [16384], P('rows'), may hold values from 0.3 to 3
- next_bricks: float32 [16384, 4096], P(('rows', 'snaps')), may hold values from -6 to 6
- brick_source: int32 [8, 64], P('rows'), may hold values from 0 to 63, each once within a row
Outputs:
- gram: float32 [4096, 4096], P('rows', 'snaps')
- next_tiles: float32 [16384, 4096], P('rows', 'snaps')
Inputs may be any that keep to these rules, and one draw needn't show every extreme that they name: Each row of brick_source is a permutation of 0 to 63.
All inputs are finite; a program needn't handle non-finite values.
Results may differ from a plain program's by a relative error of at most 0.00007.
Values sent between devices are 32-bit elements; how exact they have to be, the bound alone decides.
No kernel may reach another device: no remote copies, remote signals or barrier semaphores. Data moves between devices by JAX's collectives and lax.ppermute only.
A program may use at most 128 MiB of HBM per device.

v0:
```python
import math
import jax
import jax.numpy as jnp
from jax import lax
from jax.sharding import Mesh
from jax.sharding import PartitionSpec as P

BRICK = 32
ROWS = ("rows_0", "rows_1")
ROWS_SNAPS = ("rows_0", "rows_1", "snaps")


def scatter_axes(x, axes, dim):
    if not axes:
        return x
    nearer = lax.psum_scatter(x, axes[0], scatter_dimension=dim, tiled=True)
    return scatter_axes(nearer, axes[1:], dim)


def pair_tile(left, right):
    return lax.dot_general(
        left,
        right,
        (((0,), (0,)), ((), ())),
        precision=lax.Precision.HIGHEST,
        preferred_element_type=jnp.float32,
    )


def per_device(snapshots, weights, next_bricks, brick_source):
    width = snapshots.shape[1]
    rows_here = snapshots.shape[0]
    weighted = snapshots * weights[:, None]
    scale = jnp.float32(math.sqrt(rows_here * lax.axis_size(ROWS)))
    column = pair_tile(lax.all_gather(snapshots, "snaps", axis=1, tiled=True), weighted)
    arrived = lax.all_to_all(next_bricks, "snaps", split_axis=1, concat_axis=0, tiled=True)
    bricks = arrived.reshape(-1, BRICK, width)
    next_tiles = jnp.take(bricks, brick_source[0], axis=0).reshape(-1, width)
    summed = scatter_axes(column, ROWS, 0)
    return (summed / scale, next_tiles)


def solution(mesh):
    torus = Mesh(mesh.devices.reshape(4, 2, mesh.shape["snaps"]), ("rows_0", "rows_1", "snaps"))
    in_specs = (P(ROWS, "snaps"), P(ROWS), P(ROWS_SNAPS, None), P(ROWS, None))
    out_specs = (P(ROWS, "snaps"), P(ROWS, "snaps"))
    return jax.shard_map(
        per_device, mesh=torus, in_specs=in_specs, out_specs=out_specs, check_vma=False
    )
```

profile of v0, /device:TPU:1, one launch (start us, length us, event | category | flops | bytes accessed | tf_op | source)
XLA Modules:
  0.0 300.5 jit_solution(7561188030469283432)
XLA Ops:
  7.2 0.0 copy-start
  7.2 0.0 all-gather.2.cloned.1.call-start
  7.2 0.7 all-gather.2.cloned.1.call-update
  7.9 0.0 reduce-scatter.3.cloned.1.call-start
  8.0 175.9 %all-gather.2.cloned.1.call-done = f32[2048,4096]{1,0:T(8,128)} async-done(((f32[2048,256]{1,0:T(8,128)}), f32[2048,4096]{1,0:T(8,128)}) %all-gather.2.cloned.1.call-update) | async-done | bytes 33554448 | tf_op jit(solution)/shard_map/all_gather | solution.py:35
  183.8 0.0 copy-done
  183.8 34.3 %convolution_bitcast_fusion = f32[4096,256]{0,1:T(8,128)} fusion(f32[2048,4096]{1,0:T(8,128)} %all-gather.2.cloned.1.call-done, f32[2048,256]{1,0:T(8,128)S(1)} %copy-done, f32[2048]{0:T(1024)} %param.5), kind=kOutput, calls=%fused_computation.1 | convolution fusion | flops 25770328064 | bytes 39854080 | tf_op jit(solution)/shard_map/dot_general | solution.py:21
  218.2 0.0 copy-start.1
  218.2 0.0 reduce-scatter.3.cloned.1.call-update
  218.2 1.6 copy-done.1
  219.7 1.8 copy.8
  221.5 0.0 copy-start.2
  221.6 5.3 %all-to-all-start = ((f32[128,16,256]{0,2,1:T(8,128)}), f32[128,16,256]{0,2,1:T(8,128)S(1)}, u32[]{:S(2)}, u32[]{:S(2)}) async-start(f32[128,16,256]{0,2,1:T(8,128)} %bitcast.15), calls=%async_computation.2 | async-start | bytes 4194304 | tf_op jit(solution)/shard_map/all_to_all | solution.py:36
  226.8 0.0 reduce-scatter.5.cloned.1.call-start
  226.9 38.7 %reduce-scatter.3.cloned.1.call-done = f32[1024,256]{0,1:T(8,128)} async-done(((f32[4096,256]{0,1:T(8,128)}), f32[1024,256]{0,1:T(8,128)}) %reduce-scatter.3.cloned.1.call-update) | async-done | bytes 1048592 | tf_op jit(solution)/shard_map/reduce_scatter | solution.py:16
  265.6 0.0 reduce-scatter.5.cloned.1.call-update
  265.6 0.0 copy-done.2
  265.6 0.1 broadcast_in_dim.15
  265.7 0.1 broadcast_in_dim.16
  265.8 0.0 all-to-all-done
  265.8 1.8 copy.9
  267.7 2.3 gather_fusion
  269.9 1.7 bitcast_select_fusion
  271.6 20.3 %reduce-scatter.5.cloned.1.call-done = f32[512,256]{0,1:T(8,128)} async-done(((f32[1024,256]{0,1:T(8,128)}), f32[512,256]{0,1:T(8,128)}) %reduce-scatter.5.cloned.1.call-update) | async-done | bytes 524304 | tf_op jit(solution)/shard_map/reduce_scatter | solution.py:16
  291.9 1.1 broadcast_multiply_fusion
  293.0 1.0 copy.10
  (3 shorter events, 0.0 us)
Async XLA Ops:
  7.2 176.7 %copy-start = (f32[2048,256]{1,0:T(8,128)S(1)}, f32[2048,256]{1,0:T(8,128)}, u32[]{:S(2)}) copy-start(f32[2048,256]{1,0:T(8,128)} %param.4) | copy-start | bytes 6291460
  7.2 176.7 %all-gather.2.cloned.1.call-start = ((), (), s32[]{:S(2)}) async-start(), calls=%async_computation.3 | async-start | bytes 35651584 | tf_op jit(solution)/shard_map/all_gather | solution.py:35
  7.9 257.7 %reduce-scatter.3.cloned.1.call-start = ((), (), s32[]{:S(2)}) async-start(), calls=%async_computation.4 | async-start | bytes 5242880 | tf_op jit(solution)/shard_map/reduce_scatter | solution.py:16
  218.2 1.6 copy-start.1
  221.5 44.1 %copy-start.2 = (s32[1,64]{1,0:T(1,128)S(1)}, s32[1,64]{1,0:T(1,128)}, u32[]{:S(2)}) copy-start(s32[1,64]{1,0:T(1,128)} %param.7) | copy-start | bytes 772
  221.6 44.3 %all-to-all-start = ((f32[128,16,256]{0,2,1:T(8,128)}), f32[128,16,256]{0,2,1:T(8,128)S(1)}, u32[]{:S(2)}, u32[]{:S(2)}) async-start(f32[128,16,256]{0,2,1:T(8,128)} %bitcast.15), calls=%async_computation.2 | async-start | bytes 4194304 | tf_op jit(solution)/shard_map/all_to_all | solution.py:36
  226.8 65.1 %reduce-scatter.5.cloned.1.call-start = ((), (), s32[]{:S(2)}) async-start(), calls=%async_computation.5 | async-start | bytes 1572864 | tf_op jit(solution)/shard_map/reduce_scatter | solution.py:16
Sparse Core Ops, SparseCore 0:
  9.6 174.1 all-gather.1
  218.3 47.2 reduce-scatter.2
  268.0 23.8 reduce-scatter.4
where the time goes:
time: 301 us
  waiting for transfers between devices  236 us (78%)
  matrix products  34.3 us (11%)
  between operations  13.8 us (5%)
  local copies, waits for them, and re-layouts  8.62 us (3%)
  starting transfers between devices  5.38 us (2%)
    all_gather x1, waiting for transfers between devices, per_device(): lax.all_gather(snapshots, 'snaps', axis=1, tiled=True)  176 us
    reduce_scatter x2, waiting for transfers between devices, scatter_axes(): nearer = lax.psum_scatter(x, axes[0], scatter_dimension=dim, tiled=True)  59 us
    dot_general x1, matrix products, pair_tile(): lax.dot_general(left, right, (((0,), (0,)), ((), ())), precision=lax.Prec...  34.3 us
  transfers between devices with their start and end apart: 4, of which 3 were waited for; matrix products, arithmetic and copies ran while one was open for 3% of the time, Pallas kernels for 0%

commit v1 on v0

--- a/solution.py
+++ b/solution.py
@@ -4,10 +4,19 @@
 from jax import lax
 from jax.sharding import Mesh
 from jax.sharding import PartitionSpec as P
+from jax.lax import all_to_all, axis_size
 
 BRICK = 32
 ROWS = ("rows_0", "rows_1")
 ROWS_SNAPS = ("rows_0", "rows_1", "snaps")
+
+
+def view_the_plane(content):
+    spare = jnp.concatenate(
+        all_to_all(jnp.stack([content for _ in range(axis_size("snaps"))], axis=0), "snaps", 0, 0),
+        1,
+    )
+    return spare
 
 
 def scatter_axes(x, axes, dim):
@@ -32,7 +41,7 @@
     rows_here = snapshots.shape[0]
     weighted = snapshots * weights[:, None]
     scale = jnp.float32(math.sqrt(rows_here * lax.axis_size(ROWS)))
-    column = pair_tile(lax.all_gather(snapshots, "snaps", axis=1, tiled=True), weighted)
+    column = pair_tile(view_the_plane(snapshots), weighted)
     arrived = lax.all_to_all(next_bricks, "snaps", split_axis=1, concat_axis=0, tiled=True)
     bricks = arrived.reshape(-1, BRICK, width)
     next_tiles = jnp.take(bricks, brick_source[0], axis=0).reshape(-1, width)

time: 301 us -> 531 us (1.76)
  blocking collectives: 0 us -> 372 us
  waiting for transfers between devices: 236 us -> 60.2 us
  matrix products: 34.3 us -> 59.7 us
  local copies, waits for them, and re-layouts: 8.62 us -> 14.7 us
    all_to_all x0 -> x1, blocking collectives: none -> 372 us  [view_the_plane(): all_to_all(jnp.stack([content for _ in range(axis_size('snaps'))], axis=0...]
    all_gather x1 -> x0, waiting for transfers between devices: 176 us -> none  [per_device(): lax.all_gather(snapshots, 'snaps', axis=1, tiled=True)]
    dot_general x1, matrix products: 34.3 us -> 59.7 us  [pair_tile(): lax.dot_general(left, right, (((0,), (0,)), ((), ())), precision=lax.Prec...]
  transfers between devices with their start and end apart: 4 -> 3, of which waited for: 3 -> 2; matrix products, arithmetic and copies ran while one was open for 3% -> 1% of each run, Pallas kernels for 0% -> 0%
where the time goes in v1:
time: 531 us
  blocking collectives  372 us (70%)
  waiting for transfers between devices  60.2 us (11%)
  matrix products  59.7 us (11%)
  local copies, waits for them, and re-layouts  14.7 us (3%)
  between operations  14.1 us (3%)
  starting transfers between devices  6.88 us (1%)
    all_to_all x1, blocking collectives, view_the_plane(): all_to_all(jnp.stack([content for _ in range(axis_size('snaps'))], axis=0...  372 us
    reduce_scatter x2, waiting for transfers between devices, scatter_axes(): nearer = lax.psum_scatter(x, axes[0], scatter_dimension=dim, tiled=True)  60.1 us
    dot_general x1, matrix products, pair_tile(): lax.dot_general(left, right, (((0,), (0,)), ((), ())), precision=lax.Prec...  59.7 us
  transfers between devices with their start and end apart: 3, of which 2 were waited for; matrix products, arithmetic and copies ran while one was open for 1% of the time, Pallas kernels for 0%

profile of v1, /device:TPU:1, one launch (start us, length us, event | category | flops | bytes accessed | tf_op | source)
XLA Modules:
  0.0 530.5 jit_solution(1128492779243163851)
XLA Ops:
  7.2 0.0 reduce-scatter.3.cloned.1.call-start
  7.2 1.9 copy.9
  9.1 4.1 stack.2
  13.3 0.0 copy-start
  13.3 0.0 copy-start.2
  13.3 372.2 %all_to_all.21 = f32[16,2048,256]{1,2,0:T(8,128)} all-to-all(f32[16,2048,256]{1,2,0:T(8,128)S(1)} %stack.2), channel_id=1, replica_groups=mesh['rows_0'=4,'rows_1'=2,'snaps'=16] {'snaps'}, dimensions={0} | all-to-all | bytes 67108864 | tf_op jit(solution)/shard_map/all_to_all | solution.py:16
  385.6 0.0 copy-done
  385.6 0.0 copy-done.2
  385.6 59.7 %convolution_bitcast_fusion = f32[4096,256]{0,1:T(8,128)} fusion(f32[2048,4096]{0,1:T(8,128)} %bitcast.17, f32[2048,256]{1,0:T(8,128)S(1)} %copy-done, f32[2048]{0:T(1024)S(1)} %copy-done.2), kind=kOutput, calls=%fused_computation.1 | convolution fusion | flops 25770328064 | bytes 39854080 | tf_op jit(solution)/shard_map/dot_general | solution.py:30
  445.2 0.0 copy-start.1
  445.2 0.0 reduce-scatter.3.cloned.1.call-update
  445.3 1.6 copy-done.1
  446.8 1.8 copy.10
  448.6 0.0 copy-start.3
  448.6 6.8 %all-to-all-start.1 = ((f32[128,16,256]{0,2,1:T(8,128)}), f32[128,16,256]{0,2,1:T(8,128)S(1)}, u32[]{:S(2)}, u32[]{:S(2)}) async-start(f32[128,16,256]{0,2,1:T(8,128)} %bitcast.19), calls=%async_computation.3 | async-start | bytes 4194304 | tf_op jit(solution)/shard_map/all_to_all | solution.py:45
  455.4 0.0 reduce-scatter.5.cloned.1.call-start
  455.5 39.8 %reduce-scatter.3.cloned.1.call-done = f32[1024,256]{0,1:T(8,128)} async-done(((f32[4096,256]{0,1:T(8,128)}), f32[1024,256]{0,1:T(8,128)}) %reduce-scatter.3.cloned.1.call-update) | async-done | bytes 1048592 | tf_op jit(solution)/shard_map/reduce_scatter | solution.py:25
  495.3 0.0 reduce-scatter.5.cloned.1.call-update
  495.3 0.0 copy-done.3
  495.3 0.1 broadcast_in_dim.15
  495.4 0.1 broadcast_in_dim.16
  495.5 0.0 all-to-all-done.1
  495.5 1.8 copy.11
  497.3 2.3 gather_fusion
  499.6 1.7 bitcast_select_fusion
  501.3 20.3 %reduce-scatter.5.cloned.1.call-done = f32[512,256]{0,1:T(8,128)} async-done(((f32[1024,256]{0,1:T(8,128)}), f32[512,256]{0,1:T(8,128)}) %reduce-scatter.5.cloned.1.call-update) | async-done | bytes 524304 | tf_op jit(solution)/shard_map/reduce_scatter | solution.py:25
  521.6 1.1 broadcast_multiply_fusion
  522.7 1.0 copy.12
  (3 shorter events, 0.0 us)
Async XLA Ops:
  7.2 488.1 %reduce-scatter.3.cloned.1.call-start = ((), (), s32[]{:S(2)}) async-start(), calls=%async_computation.4 | async-start | bytes 5242880 | tf_op jit(solution)/shard_map/reduce_scatter | solution.py:25
  13.3 372.3 %copy-start = (f32[2048,256]{1,0:T(8,128)S(1)}, f32[2048,256]{1,0:T(8,128)}, u32[]{:S(2)}) copy-start(f32[2048,256]{1,0:T(8,128)} %param.4) | copy-start | bytes 6291460
  13.3 372.3 %copy-start.2 = (f32[2048]{0:T(1024)S(1)}, f32[2048]{0:T(1024)}, u32[]{:S(2)}) copy-start(f32[2048]{0:T(1024)} %param.5) | copy-start | bytes 24580
  445.2 1.6 copy-start.1
  448.6 46.7 %copy-start.3 = (s32[1,64]{1,0:T(1,128)S(1)}, s32[1,64]{1,0:T(1,128)}, u32[]{:S(2)}) copy-start(s32[1,64]{1,0:T(1,128)} %param.7) | copy-start | bytes 772
  448.6 46.9 %all-to-all-start.1 = ((f32[128,16,256]{0,2,1:T(8,128)}), f32[128,16,256]{0,2,1:T(8,128)S(1)}, u32[]{:S(2)}, u32[]{:S(2)}) async-start(f32[128,16,256]{0,2,1:T(8,128)} %bitcast.19), calls=%async_computation.3 | async-start | bytes 4194304 | tf_op jit(solution)/shard_map/all_to_all | solution.py:45
  455.4 66.2 %reduce-scatter.5.cloned.1.call-start = ((), (), s32[]{:S(2)}) async-start(), calls=%async_computation.5 | async-start | bytes 1572864 | tf_op jit(solution)/shard_map/reduce_scatter | solution.py:25
Sparse Core Ops, SparseCore 0:
  445.4 49.8 reduce-scatter.2
  497.6 23.9 reduce-scatter.4
